TPU v7x, 32 devices: a whole 2x2x4 slice. The times are simulated.
32 devices in a mesh: lat: 8 (over z, y), lon: 4 (over x, core).
Axes of the slice: x: 2, y: 2, z: 4, core: 2. Of those that a mesh axis runs over, the one named last changes fastest.
Arguments:
- raw_fields: bfloat16 [32, 160, 1440], P(('lat', 'lon')), may hold values from -6 to 6
- embed_weight: bfloat16 [32, 4, 4, 1024], replicated, may hold values from -0.25 to 0.25
- embed_bias: float32 [1024], replicated, may hold values from -3 to 3
- conv_weight: bfloat16 [3, 3, 1024, 1024], replicated, may hold values from -0.0625 to 0.0625
- conv_bias: float32 [1024], replicated, may hold values from -3 to 3
Outputs:
- features: bfloat16 [40, 360, 1024], P('lat', 'lon')
All inputs are finite; a program needn't handle non-finite values.
Results may differ from a plain program's by a relative error of at most 0.0049.
Values may be sent and summed in bfloat16 or wider, within the bound.
No kernel may reach another device: no remote copies, remote signals or barrier semaphores. Data moves between devices by JAX's collectives and lax.ppermute only.
A program may use at most 192 MiB of HBM per device.

v0:
```python
import jax
import jax.numpy as jnp
from jax import lax
from jax.sharding import PartitionSpec as P

PATCH = 4


def with_halo(value, sides, width, wrap):
    for axis, dim in sides:
        count, length = (lax.axis_size(axis), value.shape[dim])
        up = [(i, (i + 1) % count) for i in range(count if wrap else count - 1)]
        down = [(j, i) for i, j in up]
        last = lax.slice_in_dim(value, length - width, length, axis=dim)
        leading = lax.slice_in_dim(value, 0, width, axis=dim)
        before = lax.ppermute(last, axis, up)
        after = lax.ppermute(leading, axis, down)
        value = jnp.concatenate([before, value, after], axis=dim)
    return value


def per_device(raw_fields, embed_weight, embed_bias, conv_weight, conv_bias):
    lat_count = lax.axis_size("lat")
    lon_count = lax.axis_size("lon")
    var_dev, height, breadth = raw_fields.shape
    tile_height = height // lat_count
    tile_breadth = breadth // lon_count
    pieces = raw_fields.reshape(var_dev, lat_count, tile_height, lon_count, tile_breadth)
    pieces = pieces.transpose(1, 3, 0, 2, 4).reshape(
        lat_count * lon_count * var_dev, tile_height, tile_breadth
    )
    tile_block = lax.all_to_all(pieces, ("lat", "lon"), split_axis=0, concat_axis=0, tiled=True)
    patch_rows = tile_height // PATCH
    patch_cols = tile_breadth // PATCH
    grid_blocks = tile_block.reshape(-1, patch_rows, PATCH, patch_cols, PATCH)
    embedded = jnp.einsum(
        "vaibj,vijd->abd", grid_blocks, embed_weight, preferred_element_type=jnp.float32
    )
    embedded = (embedded + embed_bias).astype(jnp.bfloat16)
    channels = embedded.shape[2]
    lon_padded = with_halo(embedded, (("lon", 1),), 1, True)
    padded = with_halo(lon_padded, (("lat", 0),), 1, False)
    summed = jnp.zeros((patch_rows * patch_cols, channels), jnp.float32)
    for step_row in range(3):
        for step_col in range(3):
            window = padded[
                step_row : step_row + patch_rows, step_col : step_col + patch_cols
            ].reshape(-1, channels)
            summed = summed + jnp.dot(
                window, conv_weight[step_row, step_col], preferred_element_type=jnp.float32
            )
    summed = summed + conv_bias
    result = jax.nn.gelu(summed, approximate=False).astype(jnp.bfloat16)
    return result.reshape(patch_rows, patch_cols, channels)


def solution(mesh):
    return jax.shard_map(
        per_device,
        mesh=mesh,
        in_specs=(P(("lat", "lon"), None, None), P(), P(), P(), P()),
        out_specs=P("lat", "lon", None),
        check_vma=False,
    )
```

profile of v0, /device:TPU:0, one launch (start us, length us, event | category | flops | bytes accessed | tf_op | source)
XLA Modules:
  0.0 93.1 jit_solution(10198314950242931978)
XLA Ops:
  0.0 1.5 %reshape.41 = bf16[1,8,20,4,360]{4,3,2,1,0:T(4,128)(2,1)S(1)} reshape(bf16[1,160,1440]{2,1,0:T(8,128)(2,1)} %param.5) | data formatting | bytes 921600 | tf_op jit(solution)/shard_map/reshape | solution.py:28
  1.5 0.2 copy.27
  1.9 23.9 %all_to_all.5 = bf16[32,20,360]{2,1,0:T(8,128)(2,1)S(1)} all-to-all(bf16[32,20,360]{2,1,0:T(8,128)(2,1)S(1)} %bitcast.52), channel_id=1, replica_groups=mesh['lat'=8,'lon'=4] {'lat','lon'}, dimensions={0} | all-to-all | bytes 921600 | tf_op jit(solution)/shard_map/all_to_all | solution.py:32
  25.8 1.3 %copy.13 = bf16[32,20,360]{0,2,1:T(8,128)(2,1)S(1)} copy(bf16[32,20,360]{2,1,0:T(8,128)(2,1)S(1)} %all_to_all.5) | data formatting | bytes 921600 | tf_op jit(solution)/shard_map/all_to_all | solution.py:32
  27.2 2.8 %fusion.27 = bf16[5,90,1024]{2,1,0:T(8,128)(2,1)S(1)} fusion(bf16[32,5,4,90,4]{0,4,3,2,1:T(4,128)(2,1)S(1)} %bitcast.54, bf16[32,4,4,1024]{3,2,1,0:T(4,128)(2,1)} %param.6, f32[1024]{0:T(1024)S(1)} %copy-done.5), kind=kOutput, calls=%fused_computation.29 | convolution fusion | flops 472780800 | bytes 2435072 | tf_op jit(solution)/shard_map/vaibj,vijd->abd/dot_general | solution.py:36
  30.1 0.2 reshape.48
  30.3 1.7 %collective-permute-start.1 = (bf16[5,1,1024]{2,1,0:T(2,128)(2,1)S(1)}, bf16[5,1,1024]{2,1,0:T(2,128)(2,1)S(1)}, u32[]{:S(2)}, u32[]{:S(2)}) collective-permute-start(bf16[5,1,1024]{2,1,0:T(2,128)(2,1)S(1)} %get-tuple-element.18), channel_id=1, source_target_pairs={{1,0},{2,1},{3,2},{0,3},{5,4},{6,5},{7,6},{4,7},{9,8},{10,9},{11,1... | collective-permute-start | bytes 30728 | tf_op jit(solution)/shard_map/ppermute | solution.py:17
  32.1 4.0 %fusion.8 = f32[450,1024]{1,0:T(8,128)} fusion(bf16[450,1024]{1,0:T(8,128)(2,1)S(1)} %reshape.48, bf16[3,3,1024,1024]{3,2,1,0:T(8,128)(2,1)} %param.8), kind=kOutput, calls=%fused_computation.9 | convolution fusion | flops 943718400 | bytes 4861952 | tf_op jit(solution)/shard_map/dot_general | solution.py:49
  36.1 0.8 pad_maximum_fusion.5
  36.9 3.2 %collective-permute-start.2 = (bf16[1,92,1024]{2,1,0:T(8,128)(2,1)}, bf16[1,92,1024]{2,1,0:T(8,128)(2,1)S(1)}, u32[]{:S(2)}, u32[]{:S(2)}) collective-permute-start(bf16[1,92,1024]{2,1,0:T(8,128)(2,1)} %get-tuple-element.13), channel_id=1, source_target_pairs={{0,4},{4,8},{8,12},{12,16},{16,20},{20,24},{24,28},{1,5},{5,9},{9,... | collective-permute-start | bytes 565256 | tf_op jit(solution)/shard_map/ppermute | solution.py:16
  40.1 1.3 %collective-permute-start.3 = (bf16[1,92,1024]{2,1,0:T(8,128)(2,1)S(1)}, bf16[1,92,1024]{2,1,0:T(8,128)(2,1)S(1)}, u32[]{:S(2)}, u32[]{:S(2)}) collective-permute-start(bf16[1,92,1024]{2,1,0:T(8,128)(2,1)S(1)} %get-tuple-element.14), channel_id=1, source_target_pairs={{4,0},{8,4},{12,8},{16,12},{20,16},{24,20},{28,24},{5,1},{9,5},{13... | collective-permute-start | bytes 565256 | tf_op jit(solution)/shard_map/ppermute | solution.py:17
  41.4 0.5 pad_maximum_fusion.2
  41.9 1.1 %reshape.47 = bf16[450,1024]{1,0:T(8,128)(2,1)} reshape(bf16[5,90,1024]{2,1,0:T(8,128)(2,1)S(1)} %get-tuple-element.15) | data formatting | bytes 1843200 | tf_op jit(solution)/shard_map/reshape | solution.py:48
  43.0 4.3 %fusion.10 = f32[450,1024]{1,0:T(8,128)} fusion(bf16[450,1024]{1,0:T(8,128)(2,1)} %reshape.47, bf16[3,3,1024,1024]{3,2,1,0:T(8,128)(2,1)} %param.8), kind=kOutput, calls=%fused_computation.11 | convolution fusion | flops 943718400 | bytes 4874240 | tf_op jit(solution)/shard_map/dot_general | solution.py:49
  47.3 0.2 reshape.49
  47.6 4.0 %fusion.6 = f32[450,1024]{1,0:T(8,128)} fusion(bf16[450,1024]{1,0:T(8,128)(2,1)S(1)} %reshape.49, bf16[3,3,1024,1024]{3,2,1,0:T(8,128)(2,1)} %param.8), kind=kOutput, calls=%fused_computation.7 | convolution fusion | flops 943718400 | bytes 4861952 | tf_op jit(solution)/shard_map/dot_general | solution.py:49
  51.5 0.5 maximum_maximum_fusion
  52.0 2.5 %fusion.46 = (bf16[5,90,1024]{2,1,0:T(8,128)(2,1)}, bf16[5,90,1024]{2,1,0:T(8,128)(2,1)}, bf16[5,90,1024]{2,1,0:T(8,128)(2,1)}, bf16[5,90,1024]{2,1,0:T(8,128)(2...) fusion(bf16[6,92,1024]{2,1,0:T(8,128)(2,1)S(1)} %get-tuple-element.12, ...), kind=kLoop, calls=%fused_computation.61 | loop fusion | bytes 11059200 | tf_op jit(solution)/shard_map/slice | solution.py:46
  54.6 2.3 %reshape.52 = bf16[450,1024]{1,0:T(8,128)(2,1)} reshape(bf16[5,90,1024]{2,1,0:T(8,128)(2,1)} %get-tuple-element.5) | data formatting | bytes 1843200 | tf_op jit(solution)/shard_map/reshape | solution.py:48
  56.8 2.3 %reshape.51 = bf16[450,1024]{1,0:T(8,128)(2,1)} reshape(bf16[5,90,1024]{2,1,0:T(8,128)(2,1)} %get-tuple-element.6) | data formatting | bytes 1843200 | tf_op jit(solution)/shard_map/reshape | solution.py:48
  59.1 4.3 %fusion.2 = f32[450,1024]{1,0:T(8,128)} fusion(bf16[450,1024]{1,0:T(8,128)(2,1)} %reshape.51, bf16[3,3,1024,1024]{3,2,1,0:T(8,128)(2,1)} %param.8), kind=kOutput, calls=%fused_computation.3 | convolution fusion | flops 943718400 | bytes 4874240 | tf_op jit(solution)/shard_map/dot_general | solution.py:49
  63.4 2.3 %reshape.50 = bf16[450,1024]{1,0:T(8,128)(2,1)} reshape(bf16[5,90,1024]{2,1,0:T(8,128)(2,1)} %get-tuple-element.7) | data formatting | bytes 1843200 | tf_op jit(solution)/shard_map/reshape | solution.py:48
  65.6 4.3 %fusion.4 = f32[450,1024]{1,0:T(8,128)} fusion(bf16[450,1024]{1,0:T(8,128)(2,1)} %reshape.50, bf16[3,3,1024,1024]{3,2,1,0:T(8,128)(2,1)} %param.8), kind=kOutput, calls=%fused_computation.5 | convolution fusion | flops 943718400 | bytes 4874240 | tf_op jit(solution)/shard_map/dot_general | solution.py:49
  70.0 1.1 %reshape.44 = bf16[450,1024]{1,0:T(8,128)(2,1)} reshape(bf16[5,90,1024]{2,1,0:T(8,128)(2,1)S(1)} %get-tuple-element.19) | data formatting | bytes 1843200 | tf_op jit(solution)/shard_map/reshape | solution.py:48
  71.1 4.4 %fusion.16 = f32[450,1024]{1,0:T(8,128)} fusion(bf16[450,1024]{1,0:T(8,128)(2,1)} %reshape.44, bf16[3,3,1024,1024]{3,2,1,0:T(8,128)(2,1)} %param.8), kind=kOutput, calls=%fused_computation.17 | convolution fusion | flops 943718400 | bytes 4874240 | tf_op jit(solution)/shard_map/dot_general | solution.py:49
  75.5 0.2 reshape.46
  75.7 4.0 %fusion.12 = f32[450,1024]{1,0:T(8,128)} fusion(bf16[450,1024]{1,0:T(8,128)(2,1)S(1)} %reshape.46, bf16[3,3,1024,1024]{3,2,1,0:T(8,128)(2,1)} %param.8), kind=kOutput, calls=%fused_computation.13 | convolution fusion | flops 943718400 | bytes 4861952 | tf_op jit(solution)/shard_map/dot_general | solution.py:49
  79.7 0.2 reshape.45
  79.9 2.9 %fusion.14 = f32[450,1024]{1,0:T(8,128)S(1)} fusion(bf16[450,1024]{1,0:T(8,128)(2,1)S(1)} %reshape.45, bf16[3,3,1024,1024]{3,2,1,0:T(8,128)(2,1)} %param.8), kind=kOutput, calls=%fused_computation.15 | convolution fusion | flops 943718400 | bytes 4861952 | tf_op jit(solution)/shard_map/dot_general | solution.py:49
  82.9 0.6 copy-done.9
  83.5 8.5 %fusion.32 = bf16[450,1024]{1,0:T(8,128)(2,1)S(1)} fusion(f32[450,1024]{1,0:T(8,128)} %fusion.2, f32[450,1024]{1,0:T(8,128)} %fusion.4, f32[450,1024]{1,0:T(8,128)S(1)} %copy-done.9, f32[450,1024]{1,0:T(8,128)S(1)} %copy-done.7, f32[450,1024]{1,0:T(8,128)S(1)} %copy-done.8, f32[450,1024]{1,0:T(8,128)} %fusion.12, f32[450,1024]{1,0:T(8,128)} %fusion.16, ...), kind=kOutput, calls=%fused_computation.34 | convolution fusion | flops 977817600 | bytes 18788352 | tf_op jit(solution)/shard_map/dot_general | solution.py:49
  91.9 1.2 %reshape.53 = bf16[5,90,1024]{2,1,0:T(8,128)(2,1)} reshape(bf16[450,1024]{1,0:T(8,128)(2,1)S(1)} %fusion.32) | data formatting | bytes 1843200 | tf_op jit(solution)/shard_map/reshape | solution.py:54
  (26 shorter events, 0.4 us)
Async XLA Ops:
  1.9 25.3 %copy-start.5 = (f32[1024]{0:T(1024)S(1)}, f32[1024]{0:T(1024)}, u32[]{:S(2)}) copy-start(f32[1024]{0:T(1024)} %param.7) | copy-start | bytes 12292
  30.3 5.8 %collective-permute-start = (bf16[5,1,1024]{2,1,0:T(2,128)(2,1)S(1)}, bf16[5,1,1024]{2,1,0:T(2,128)(2,1)S(1)}, u32[]{:S(2)}, u32[]{:S(2)}) collective-permute-start(bf16[5,1,1024]{2,1,0:T(2,128)(2,1)S(1)} %get-tuple-element.17), channel_id=1, source_target_pairs={{0,1},{1,2},{2,3},{3,0},{4,5},{5,6},{6,7},{7,4},{8,9},{9,10},{10,1... | collective-permute-start | bytes 30728 | tf_op jit(solution)/shard_map/ppermute | solution.py:16
  30.3 5.7 %collective-permute-start.1 = (bf16[5,1,1024]{2,1,0:T(2,128)(2,1)S(1)}, bf16[5,1,1024]{2,1,0:T(2,128)(2,1)S(1)}, u32[]{:S(2)}, u32[]{:S(2)}) collective-permute-start(bf16[5,1,1024]{2,1,0:T(2,128)(2,1)S(1)} %get-tuple-element.18), channel_id=1, source_target_pairs={{1,0},{2,1},{3,2},{0,3},{5,4},{6,5},{7,6},{4,7},{9,8},{10,9},{11,1... | collective-permute-start | bytes 30728 | tf_op jit(solution)/shard_map/ppermute | solution.py:17
  36.1 5.8 %copy-start.1 = (bf16[5,1,1024]{2,1,0:T(2,128)(2,1)}, bf16[5,1,1024]{2,1,0:T(2,128)(2,1)S(1)}, u32[]{:S(2)}) copy-start(bf16[5,1,1024]{2,1,0:T(2,128)(2,1)S(1)} %collective-permute-done) | copy-start | bytes 30724
  36.1 5.8 %copy-start.3 = (bf16[5,1,1024]{2,1,0:T(2,128)(2,1)}, bf16[5,1,1024]{2,1,0:T(2,128)(2,1)S(1)}, u32[]{:S(2)}) copy-start(bf16[5,1,1024]{2,1,0:T(2,128)(2,1)S(1)} %collective-permute-done.1) | copy-start | bytes 30724
  36.9 14.6 %collective-permute-start.2 = (bf16[1,92,1024]{2,1,0:T(8,128)(2,1)}, bf16[1,92,1024]{2,1,0:T(8,128)(2,1)S(1)}, u32[]{:S(2)}, u32[]{:S(2)}) collective-permute-start(bf16[1,92,1024]{2,1,0:T(8,128)(2,1)} %get-tuple-element.13), channel_id=1, source_target_pairs={{0,4},{4,8},{8,12},{12,16},{16,20},{20,24},{24,28},{1,5},{5,9},{9,... | collective-permute-start | bytes 565256 | tf_op jit(solution)/shard_map/ppermute | solution.py:16
  40.1 11.4 %collective-permute-start.3 = (bf16[1,92,1024]{2,1,0:T(8,128)(2,1)S(1)}, bf16[1,92,1024]{2,1,0:T(8,128)(2,1)S(1)}, u32[]{:S(2)}, u32[]{:S(2)}) collective-permute-start(bf16[1,92,1024]{2,1,0:T(8,128)(2,1)S(1)} %get-tuple-element.14), channel_id=1, source_target_pairs={{4,0},{8,4},{12,8},{16,12},{20,16},{24,20},{28,24},{5,1},{9,5},{13... | collective-permute-start | bytes 565256 | tf_op jit(solution)/shard_map/ppermute | solution.py:17
  47.5 4.0 %copy-start.2 = (bf16[5,1,1024]{2,1,0:T(2,128)(2,1)S(1)}, bf16[5,1,1024]{2,1,0:T(2,128)(2,1)}, u32[]{:S(2)}) copy-start(bf16[5,1,1024]{2,1,0:T(2,128)(2,1)} %copy-done.1) | copy-start | bytes 30724
  47.5 4.0 %copy-start.4 = (bf16[5,1,1024]{2,1,0:T(2,128)(2,1)S(1)}, bf16[5,1,1024]{2,1,0:T(2,128)(2,1)}, u32[]{:S(2)}) copy-start(bf16[5,1,1024]{2,1,0:T(2,128)(2,1)} %copy-done.3) | copy-start | bytes 30724
  79.9 2.9 %copy-start = (bf16[450,1024]{1,0:T(8,128)(2,1)S(1)}, bf16[450,1024]{1,0:T(8,128)(2,1)}, u32[]{:S(2)}) copy-start(bf16[450,1024]{1,0:T(8,128)(2,1)} %reshape.52) | copy-start | bytes 2764804
  79.9 2.9 %copy-start.6 = (f32[1024]{0:T(1024)S(1)}, f32[1024]{0:T(1024)}, u32[]{:S(2)}) copy-start(f32[1024]{0:T(1024)} %param.9) | copy-start | bytes 12292
  79.9 2.9 %copy-start.7 = (f32[450,1024]{1,0:T(8,128)S(1)}, f32[450,1024]{1,0:T(8,128)}, u32[]{:S(2)}) copy-start(f32[450,1024]{1,0:T(8,128)} %fusion.8) | copy-start | bytes 5529604
  79.9 3.0 %copy-start.8 = (f32[450,1024]{1,0:T(8,128)S(1)}, f32[450,1024]{1,0:T(8,128)}, u32[]{:S(2)}) copy-start(f32[450,1024]{1,0:T(8,128)} %fusion.10) | copy-start | bytes 5529604
  79.9 3.5 %copy-start.9 = (f32[450,1024]{1,0:T(8,128)S(1)}, f32[450,1024]{1,0:T(8,128)}, u32[]{:S(2)}) copy-start(f32[450,1024]{1,0:T(8,128)} %fusion.6) | copy-start | bytes 5529604
where the time goes:
time: 94.2 us; the launch traced here: 93.1 us
  matrix products  43.4 us (46%)
  blocking collectives  23.9 us (25%)
  local copies, waits for them, and re-layouts  17.5 us (19%)
  starting transfers between devices  6.3 us (7%)
  other arithmetic  1.77 us (2%)
    dot_general x9, matrix products, per_device(): jnp.dot(window, conv_weight[step_row, step_col], preferred_element_type=j...  40.5 us
    all_to_all x1, blocking collectives, per_device(): lax.all_to_all(pieces, ('lat', 'lon'), split_axis=0, concat_axis=0, tiled...  23.9 us
    reshape x9, local copies, waits for them, and re-layouts, per_device(): window = padded[step_row:step_row + patch_rows, step_col:step_col + patch...  9.87 us
    ppermute x2, starting transfers between devices, with_halo(): before = lax.ppermute(last, axis, up)  3.27 us
    ppermute x2, starting transfers between devices, with_halo(): after = lax.ppermute(leading, axis, down)  3.02 us
    dot_general x1, matrix products, per_device(): jnp.einsum('vaibj,vijd->abd', grid_blocks, embed_weight, preferred_elemen...  2.83 us
    slice x1, local copies, waits for them, and re-layouts, per_device(): padded[step_row:step_row + patch_rows, step_col:step_col + patch_cols]  2.52 us
  transfers between devices with their start and end apart: 4, of which 0 were waited for; matrix products, arithmetic and copies ran while one was open for 15% of the time, Pallas kernels for 0%

commit v1 on v0

--- a/solution.py
+++ b/solution.py
@@ -1,9 +1,14 @@
+import functools
+
 import jax
 import jax.numpy as jnp
 from jax import lax
+from jax.experimental import pallas as pl
+from jax.experimental.pallas import tpu as pltpu
 from jax.sharding import PartitionSpec as P
 
 PATCH = 4
+LANES = 128
 
 
 def with_halo(value, sides, width, wrap):
@@ -19,7 +24,7 @@
     return value
 
 
-def per_device(raw_fields, embed_weight, embed_bias, conv_weight, conv_bias):
+def two_stages(raw_fields, embed_weight, embed_bias, conv_weight, conv_bias):
     lat_count = lax.axis_size("lat")
     lon_count = lax.axis_size("lon")
     var_dev, height, breadth = raw_fields.shape
@@ -54,6 +59,169 @@
     return result.reshape(patch_rows, patch_cols, channels)
 
 
+def windows_kernel(raw_ref, out_ref, *, lat_count, lon_count, tile_rows, tile_breadth):
+    height, breadth = raw_ref.shape[1:]
+    span = tile_breadth + 2 * PATCH
+    patches_high = height // PATCH
+    rows = tile_rows + 2
+    raw = raw_ref[0]
+    for lon in range(lon_count):
+        first = lon * tile_breadth - PATCH
+        last = first + span
+        if first < 0:
+            window = jnp.concatenate([raw[:, first:], raw[:, :last]], axis=1)
+        elif last > breadth:
+            window = jnp.concatenate([raw[:, first:], raw[:, : last - breadth]], axis=1)
+        else:
+            window = raw[:, first:last]
+        for patch_row in range(patches_high):
+            piece = window[PATCH * patch_row : PATCH * (patch_row + 1)]
+            for lat in range(lat_count):
+                for step in range(rows):
+                    wanted = lat * tile_rows - 1 + step
+                    if min(max(wanted, 0), patches_high - 1) == patch_row:
+                        out_ref[lat * lon_count + lon, step] = piece
+
+
+def compose_kernel(embed_ref, bias_ref, conv_ref, weight_ref, shift_ref):
+    weight_ref[0] = jnp.dot(
+        embed_ref[...], conv_ref[0], preferred_element_type=jnp.float32
+    ).astype(weight_ref.dtype)
+    rest = bias_ref[...]
+    shift = None
+    for _ in range(3):
+        part = rest.astype(conv_ref.dtype)
+        rest = rest - part.astype(jnp.float32)
+        term = jnp.dot(part, conv_ref[0], preferred_element_type=jnp.float32)
+        shift = term if shift is None else shift + term
+    shift_ref[0] = shift
+
+
+def tokens_kernel(
+    edge_ref, tile_ref, weight_ref, bias_ref, out_ref, turned_ref, cells_ref, *, pitch, block
+):
+    variables, rows, _, span = tile_ref.shape
+    tile_rows, tile_cols, channels = out_ref.shape
+    depth = variables * PATCH
+    steps = 3 * PATCH
+    for row in range(rows):
+        cells = tile_ref[:, row].astype(jnp.float32).reshape(depth, span)
+        if row == 0:
+            cells = cells * edge_ref[0]
+        if row == rows - 1:
+            cells = cells * edge_ref[1]
+        turned_ref[row, :span] = cells.T
+        for step in range(steps):
+            picked = turned_ref[row, pl.ds(step, pitch, stride=PATCH), :]
+            cells_ref[row * pitch : (row + 1) * pitch, step * depth : (step + 1) * depth] = (
+                picked.astype(cells_ref.dtype)
+            )
+    many = tile_rows * pitch
+    for first in range(0, channels, block):
+        total = None
+        for tap_row in range(3):
+            part = jnp.dot(
+                cells_ref[tap_row * pitch : tap_row * pitch + many],
+                weight_ref[
+                    tap_row * steps * depth : (tap_row + 1) * steps * depth, first : first + block
+                ],
+                preferred_element_type=jnp.float32,
+            )
+            total = part if total is None else total + part
+        for row in range(tile_rows):
+            kind = 0 if row == 0 else 2 if row == tile_rows - 1 else 1
+            value = total[row * pitch : row * pitch + tile_cols]
+            value = value + bias_ref[kind : kind + 1, first : first + block]
+            value = 0.5 * value * (1.0 + lax.erf(value * (0.5**0.5)))
+            out_ref[row, :, first : first + block] = value.astype(out_ref.dtype)
+
+
+def one_stage(raw_fields, embed_weight, embed_bias, conv_weight, conv_bias):
+    lat_count = lax.axis_size("lat")
+    lon_count = lax.axis_size("lon")
+    devices = lat_count * lon_count
+    _, height, breadth = raw_fields.shape
+    variables, _, _, channels = embed_weight.shape
+    tile_rows = height // lat_count // PATCH
+    tile_breadth = breadth // lon_count
+    tile_cols = tile_breadth // PATCH
+    rows = tile_rows + 2
+    span = tile_breadth + 2 * PATCH
+    depth = variables * PATCH
+    cells = depth * PATCH
+    pitch = -(-(tile_cols + 2) // 16) * 16
+    lowest = jnp.bfloat16
+
+    pieces = pl.pallas_call(
+        functools.partial(
+            windows_kernel,
+            lat_count=lat_count,
+            lon_count=lon_count,
+            tile_rows=tile_rows,
+            tile_breadth=tile_breadth,
+        ),
+        out_shape=jax.ShapeDtypeStruct((devices, rows, PATCH, span), lowest),
+        name="windows",
+    )(raw_fields)
+    tile = lax.all_to_all(pieces, ("lat", "lon"), split_axis=0, concat_axis=0, tiled=True)
+
+    turned = embed_weight.transpose(2, 0, 1, 3).reshape(cells, channels)
+    bias_rows = jnp.broadcast_to(embed_bias, (8, channels))
+    taps = conv_weight.reshape(9, channels, channels)
+    weight, shift = pl.pallas_call(
+        compose_kernel,
+        grid=(9,),
+        in_specs=[
+            pl.BlockSpec((cells, channels), lambda t: (0, 0)),
+            pl.BlockSpec((8, channels), lambda t: (0, 0)),
+            pl.BlockSpec((1, channels, channels), lambda t: (t, 0, 0)),
+        ],
+        out_specs=[
+            pl.BlockSpec((1, cells, channels), lambda t: (t, 0, 0)),
+            pl.BlockSpec((1, 8, channels), lambda t: (t, 0, 0)),
+        ],
+        out_shape=[
+            jax.ShapeDtypeStruct((9, cells, channels), lowest),
+            jax.ShapeDtypeStruct((9, 8, channels), jnp.float32),
+        ],
+        name="compose",
+    )(turned, bias_rows, taps)
+    row_shift = shift[:, 0].reshape(3, 3, channels).sum(axis=1)
+    lat = lax.axis_index("lat")
+    above = jnp.where(lat > 0, 1.0, 0.0).astype(jnp.float32)
+    below = jnp.where(lat < lat_count - 1, 1.0, 0.0).astype(jnp.float32)
+    middle = conv_bias + row_shift[1]
+    both = middle + row_shift[0] + row_shift[2]
+    top = middle + above * row_shift[0] + row_shift[2]
+    bottom = middle + row_shift[0] + below * row_shift[2]
+    biases = jnp.stack([top, both, bottom])
+    edges = jnp.stack([above, below])
+
+    return pl.pallas_call(
+        functools.partial(tokens_kernel, pitch=pitch, block=2 * LANES),
+        in_specs=[
+            pl.BlockSpec(memory_space=pltpu.SMEM),
+            pl.BlockSpec(memory_space=pltpu.VMEM),
+            pl.BlockSpec(memory_space=pltpu.VMEM),
+            pl.BlockSpec(memory_space=pltpu.VMEM),
+        ],
+        out_specs=pl.BlockSpec(memory_space=pltpu.VMEM),
+        out_shape=jax.ShapeDtypeStruct((tile_rows, tile_cols, channels), lowest),
+        scratch_shapes=[
+            pltpu.VMEM((rows, PATCH * pitch + 3 * PATCH, depth), jnp.float32),
+            pltpu.VMEM((rows * pitch, 3 * cells), lowest),
+        ],
+        name="tokens",
+    )(edges, tile, weight.reshape(9 * cells, channels), biases)
+
+
+def per_device(raw_fields, embed_weight, embed_bias, conv_weight, conv_bias):
+    variables, _, _, channels = embed_weight.shape
+    if raw_fields.shape[0] == 1 and variables * PATCH * PATCH <= channels:
+        return one_stage(raw_fields, embed_weight, embed_bias, conv_weight, conv_bias)
+    return two_stages(raw_fields, embed_weight, embed_bias, conv_weight, conv_bias)
+
+
 def solution(mesh):
     return jax.shard_map(
         per_device,

time: 94.2 us -> 48 us (0.51)
  matrix products: 43.4 us -> 0 us
  Pallas kernels: 0 us -> 32.8 us
  blocking collectives: 23.9 us -> 0 us
  local copies, waits for them, and re-layouts: 17.5 us -> 6.1 us
  starting transfers between devices: 6.3 us -> 7.33 us
    dot_general x10 -> x0, matrix products: 43.4 us -> none  [the longest x9 40.5 us: per_device(): jnp.dot(window, conv_weight[step_row, step_col], preferred_element_type=j...]
    pallas_call x0 -> x3, Pallas kernels: none -> 32.8 us  [the longest x1 20.8 us: one_stage(): pl.pallas_call(compose_kernel, grid=(9,), in_specs=[pl.BlockSpec((cells,...]
    all_to_all x1 -> x0, blocking collectives: 23.9 us -> none  [per_device(): lax.all_to_all(pieces, ('lat', 'lon'), split_axis=0, concat_axis=0, tiled...]
    reshape x13 -> x1, local copies, waits for them, and re-layouts: 12.9 us -> 1.11 us  [one_stage(): turned = embed_weight.transpose(2, 0, 1, 3).reshape(cells, channels)]
    all_to_all x0 -> x1, starting transfers between devices: none -> 7.33 us  [one_stage(): lax.all_to_all(pieces, ('lat', 'lon'), split_axis=0, concat_axis=0, tiled...]
    ppermute x4 -> x0, starting transfers between devices: 6.3 us -> none  [the longest x2 3.27 us: with_halo(): before = lax.ppermute(last, axis, up)]
    transpose x0 -> x1, local copies, waits for them, and re-layouts: none -> 1.77 us  [one_stage(): turned = embed_weight.transpose(2, 0, 1, 3).reshape(cells, channels)]
    slice x2, local copies, waits for them, and re-layouts: 2.56 us -> 1.06 us  [the longest x1 1.05 us: one_stage(): row_shift = shift[:, 0].reshape(3, 3, channels).sum(axis=1)]
  transfers between devices with their start and end apart: 4 -> 1, of which waited for: 0 -> 0; matrix products, arithmetic and copies ran while one was open for 15% -> 14% of each run, Pallas kernels for 0% -> 44%
where the time goes in v1:
time: 48 us; the launch traced here: 47.7 us
  Pallas kernels  32.8 us (68%)
  starting transfers between devices  7.33 us (15%)
  local copies, waits for them, and re-layouts  6.1 us (13%)
  other arithmetic  1.31 us (3%)
    pallas_call x1, Pallas kernels, one_stage(): pl.pallas_call(compose_kernel, grid=(9,), in_specs=[pl.BlockSpec((cells,...  20.8 us
    pallas_call x1, Pallas kernels, one_stage(): pl.pallas_call(functools.partial(tokens_kernel, pitch=pitch, block=2 * LA...  9.88 us
    all_to_all x1, starting transfers between devices, one_stage(): lax.all_to_all(pieces, ('lat', 'lon'), split_axis=0, concat_axis=0, tiled...  7.33 us
    pallas_call x1, Pallas kernels, one_stage(): pl.pallas_call(functools.partial(windows_kernel, lat_count=lat_count, lon...  2.16 us
    transpose x1, local copies, waits for them, and re-layouts, one_stage(): turned = embed_weight.transpose(2, 0, 1, 3).reshape(cells, channels)  1.77 us
    broadcast_in_dim x1, local copies, waits for them, and re-layouts, one_stage(): bias_rows = jnp.broadcast_to(embed_bias, (8, channels))  1.29 us
    reshape x1, local copies, waits for them, and re-layouts, one_stage(): turned = embed_weight.transpose(2, 0, 1, 3).reshape(cells, channels)  1.11 us
    slice x1, local copies, waits for them, and re-layouts, one_stage(): row_shift = shift[:, 0].reshape(3, 3, channels).sum(axis=1)  1.05 us
  transfers between devices with their start and end apart: 1, of which 0 were waited for; matrix products, arithmetic and copies ran while one was open for 14% of the time, Pallas kernels for 44%

profile of v1, /device:TPU:0, one launch (start us, length us, event | category | flops | bytes accessed | tf_op | source)
XLA Modules:
  0.0 47.7 jit_solution(11763280215606303660)
XLA Ops:
  0.0 0.0 copy-start.1
  0.0 2.2 %windows.1 = bf16[32,7,4,368]{3,2,1,0:T(4,128)(2,1)} custom-call(bf16[1,160,1440]{2,1,0:T(8,128)(2,1)} %raw_ref.1), custom_call_target="tpu_custom_call" | custom-call | tf_op jit(solution)/shard_map/windows/pallas_call | solution.py:155
  2.2 7.3 %all-to-all-start = ((bf16[32,7,4,368]{3,2,1,0:T(4,128)(2,1)}), bf16[32,7,4,368]{3,2,1,0:T(4,128)(2,1)S(1)}, u32[]{:S(2)}, u32[]{:S(2)}) async-start(bf16[32,7,4,368]{3,2,1,0:T(4,128)(2,1)} %windows.1), calls=%async_computation | async-start | bytes 1376256 | tf_op jit(solution)/shard_map/all_to_all | solution.py:166
  9.5 1.8 %copy.6 = bf16[4,32,4,1024]{3,2,1,0:T(4,128)(2,1)S(1)} copy(bf16[4,32,4,1024]{3,0,2,1:T(4,128)(2,1)} %bitcast.13) | data formatting | bytes 2097152 | tf_op jit(solution)/shard_map/transpose | solution.py:168
  11.3 1.1 %reshape.9.embed_ref = bf16[512,1024]{1,0:T(8,128)(2,1)} reshape(bf16[4,32,4,1024]{3,2,1,0:T(4,128)(2,1)S(1)} %copy.6) | data formatting | bytes 2097152 | tf_op jit(solution)/shard_map/reshape | solution.py:168
  12.4 1.3 %broadcast_in_dim.3.bias_ref = f32[8,1024]{1,0:T(8,128)} broadcast(f32[1024]{0:T(1024)} %param.7), dimensions={1} | broadcast | bytes 36864 | tf_op jit(solution)/shard_map/broadcast_in_dim | solution.py:169
  13.7 20.8 %compose.1 = (bf16[9,512,1024]{2,1,0:T(8,128)(2,1)}, f32[9,8,1024]{2,1,0:T(8,128)}) custom-call(bf16[512,1024]{1,0:T(8,128)(2,1)} %reshape.9.embed_ref, f32[8,1024]{1,0:T(8,128)} %broadcast_in_dim.3.bias_ref, bf16[9,1024,1024]{2,1,0:T(8,128)(2,1)} %bitcast.11), custom_call_target="tpu_custom_call" | custom-call | tf_op jit(solution)/shard_map/compose/pallas_call | solution.py:171
  34.5 1.1 %slice_reduce_fusion = f32[9,1024]{1,0:T(8,128)S(1)} fusion(f32[9,8,1024]{2,1,0:T(8,128)} %get-tuple-element.8), kind=kLoop, calls=%fused_computation | loop fusion | bytes 73728 | tf_op jit(solution)/shard_map/slice | solution.py:189
  35.6 0.6 %pad_maximum_fusion.1.edge_ref = f32[2]{0:T(128)} fusion(f32[1]{0:T(128)} %bitcast.1, f32[1]{0:T(128)} %bitcast), kind=kLoop, calls=%fused_computation.5 | loop fusion | flops 2 | bytes 16 | tf_op jit(solution)/shard_map/stack | solution.py:198
  36.3 0.0 copy-done.1
  36.3 0.6 %pad_maximum_fusion.bias_ref = f32[3,1024]{1,0:T(4,128)} fusion(f32[1,1024]{1,0:T(1,128)S(1)} %bitcast.15, f32[1,1024]{1,0:T(1,128)S(1)} %bitcast.16, f32[1,1024]{1,0:T(1,128)S(1)} %bitcast.14), kind=kLoop, calls=%fused_computation.1 | loop fusion | flops 6144 | bytes 24576 | tf_op jit(solution)/shard_map/stack | solution.py:197
  36.9 0.0 all-to-all-done.tile_ref
  36.9 0.0 copy-start
  36.9 0.9 %copy-done = bf16[32,7,4,368]{3,2,1,0:T(4,128)(2,1)} copy-done((bf16[32,7,4,368]{3,2,1,0:T(4,128)(2,1)}, bf16[32,7,4,368]{3,2,1,0:T(4,128)(2,1)S(1)}, u32[]{:S(2)}) %copy-start) | copy-done | bytes 659480
  37.8 9.9 %tokens.1 = bf16[5,90,1024]{2,1,0:T(8,128)(2,1)} custom-call(f32[2]{0:T(128)} %pad_maximum_fusion.1.edge_ref, bf16[32,7,4,368]{3,2,1,0:T(4,128)(2,1)} %copy-done, bf16[4608,1024]{1,0:T(8,128)(2,1)} %bitcast.12, f32[3,1024]{1,0:T(4,128)} %pad_maximum_fusion.bias_ref), custom_call_target="tpu_custom_call" | custom-call | tf_op jit(solution)/shard_map/tokens/pallas_call | solution.py:200
  (4 shorter events, 0.1 us)
Async XLA Ops:
  0.0 36.3 %copy-start.1 = (f32[1024]{0:T(1024)S(1)}, f32[1024]{0:T(1024)}, u32[]{:S(2)}) copy-start(f32[1024]{0:T(1024)} %param.9) | copy-start | bytes 12292
  2.2 34.7 %all-to-all-start = ((bf16[32,7,4,368]{3,2,1,0:T(4,128)(2,1)}), bf16[32,7,4,368]{3,2,1,0:T(4,128)(2,1)S(1)}, u32[]{:S(2)}, u32[]{:S(2)}) async-start(bf16[32,7,4,368]{3,2,1,0:T(4,128)(2,1)} %windows.1), calls=%async_computation | async-start | bytes 1376256 | tf_op jit(solution)/shard_map/all_to_all | solution.py:166
  36.9 0.9 %copy-start = (bf16[32,7,4,368]{3,2,1,0:T(4,128)(2,1)}, bf16[32,7,4,368]{3,2,1,0:T(4,128)(2,1)S(1)}, u32[]{:S(2)}) copy-start(bf16[32,7,4,368]{3,2,1,0:T(4,128)(2,1)S(1)} %all-to-all-done.tile_ref) | copy-start | bytes 1978372

commit v2 on v1

--- a/solution.py
+++ b/solution.py
@@ -83,57 +83,152 @@
                         out_ref[lat * lon_count + lon, step] = piece
 
 
-def compose_kernel(embed_ref, bias_ref, conv_ref, weight_ref, shift_ref):
-    weight_ref[0] = jnp.dot(
-        embed_ref[...], conv_ref[0], preferred_element_type=jnp.float32
-    ).astype(weight_ref.dtype)
+def compose_kernel(
+    embed_ref,
+    bias_ref,
+    conv_hbm,
+    near_ref,
+    far_hbm,
+    shift_ref,
+    plain_ref,
+    left_ref,
+    taps_ref,
+    made_ref,
+    arrived,
+    left,
+):
+    taps = conv_hbm.shape[0]
+    near = near_ref.shape[0]
+    parts, cells, _ = plain_ref.shape
+    depth = cells // PATCH
+    rim = left_ref.shape[0] - cells
+
+    def fetch(tap):
+        return pltpu.make_async_copy(conv_hbm.at[tap], taps_ref.at[tap], arrived.at[tap])
+
+    def send(tap):
+        return pltpu.make_async_copy(made_ref.at[tap], far_hbm.at[tap], left.at[tap])
+
+    for tap in range(taps):
+        fetch(tap).start()
     rest = bias_ref[...]
-    shift = None
-    for _ in range(3):
-        part = rest.astype(conv_ref.dtype)
-        rest = rest - part.astype(jnp.float32)
-        term = jnp.dot(part, conv_ref[0], preferred_element_type=jnp.float32)
-        shift = term if shift is None else shift + term
-    shift_ref[0] = shift
+    lines = lax.broadcasted_iota(jnp.int32, (rim, rest.shape[1]), 0)
+    below = jnp.zeros(lines.shape, jnp.float32)
+    for line in range(3):
+        part = rest.astype(left_ref.dtype).astype(jnp.float32)
+        below = jnp.where(lines == line, part, below)
+        rest = rest - part
+    left_ref[cells:] = below.astype(left_ref.dtype)
+    for part in range(parts):
+        lanes = slice(part * LANES, (part + 1) * LANES)
+        plain_ref[part] = embed_ref[..., lanes].astype(jnp.float32).reshape(cells, LANES)
+        for step in range(PATCH):
+            left_ref[step * depth : (step + 1) * depth, lanes] = plain_ref[
+                part, pl.ds(step, depth, stride=PATCH), :
+            ].astype(left_ref.dtype)
+    shift_ref[...] = jnp.zeros_like(shift_ref)
+
+    def compose(tap, keep):
+        fetch(tap).wait()
+        both = jnp.dot(left_ref[...], taps_ref[tap], preferred_element_type=jnp.float32)
+        shift_ref[tap // 3] += jnp.broadcast_to(
+            both[cells:].sum(axis=0, keepdims=True), shift_ref.shape[1:]
+        )
+        keep(both[:cells].astype(far_hbm.dtype))
+
+    def compose_near(tap, carry):
+        def keep(value):
+            near_ref[tap] = value
+
+        compose(tap, keep)
+        return carry
+
+    def compose_far(tap, carry):
+        def keep(value):
+            made_ref[tap] = value
+            send(tap).start()
+
+        compose(tap + near, keep)
+        return carry
+
+    lax.fori_loop(0, near, compose_near, None)
+    lax.fori_loop(0, taps - near, compose_far, None)
+    for tap in range(taps - near):
+        send(tap).wait()
 
 
 def tokens_kernel(
-    edge_ref, tile_ref, weight_ref, bias_ref, out_ref, turned_ref, cells_ref, *, pitch, block
+    tile_ref,
+    near_ref,
+    far_hbm,
+    shift_ref,
+    bias_ref,
+    out_ref,
+    far_ref,
+    turned_ref,
+    cells_ref,
+    total_ref,
+    arrived,
+    *,
+    pitch,
+    block,
 ):
     variables, rows, _, span = tile_ref.shape
     tile_rows, tile_cols, channels = out_ref.shape
     depth = variables * PATCH
+    cells = depth * PATCH
     steps = 3 * PATCH
+    near = near_ref.shape[0]
+    bounds = (0, 3 - near, 6 - near, 9 - near)
+
+    def fetch(tap_row):
+        taps = pl.ds(bounds[tap_row], bounds[tap_row + 1] - bounds[tap_row])
+        return pltpu.make_async_copy(far_hbm.at[taps], far_ref.at[taps], arrived.at[tap_row])
+
+    for tap_row in range(3):
+        fetch(tap_row).start()
+    lat = lax.axis_index("lat")
+    above = jnp.where(lat > 0, 1.0, 0.0).astype(jnp.float32)
+    below = jnp.where(lat < lax.axis_size("lat") - 1, 1.0, 0.0).astype(jnp.float32)
     for row in range(rows):
-        cells = tile_ref[:, row].astype(jnp.float32).reshape(depth, span)
+        tile = tile_ref[:, row].astype(jnp.float32).reshape(depth, span)
         if row == 0:
-            cells = cells * edge_ref[0]
+            tile = tile * above
         if row == rows - 1:
-            cells = cells * edge_ref[1]
-        turned_ref[row, :span] = cells.T
+            tile = tile * below
+        turned_ref[row, :span] = tile.T
         for step in range(steps):
             picked = turned_ref[row, pl.ds(step, pitch, stride=PATCH), :]
             cells_ref[row * pitch : (row + 1) * pitch, step * depth : (step + 1) * depth] = (
                 picked.astype(cells_ref.dtype)
             )
-    many = tile_rows * pitch
+
+    def product(tap_row, first, weight):
+        count = weight.shape[0]
+        left = cells_ref[
+            tap_row * pitch : (tap_row + tile_rows) * pitch, first * cells : (first + count) * cells
+        ]
+        right = weight.reshape(count * cells, weight.shape[2])
+        return jnp.dot(left, right, preferred_element_type=jnp.float32)
+
+    total_ref[...] = product(0, 0, near_ref[...])
+    fetch(0).wait()
+    total_ref[...] += product(0, near, far_ref[bounds[0] : bounds[1]])
+    fetch(1).wait()
+    total_ref[...] += product(1, 0, far_ref[bounds[1] : bounds[2]])
+    fetch(2).wait()
     for first in range(0, channels, block):
-        total = None
-        for tap_row in range(3):
-            part = jnp.dot(
-                cells_ref[tap_row * pitch : tap_row * pitch + many],
-                weight_ref[
-                    tap_row * steps * depth : (tap_row + 1) * steps * depth, first : first + block
-                ],
-                preferred_element_type=jnp.float32,
-            )
-            total = part if total is None else total + part
+        lanes = slice(first, first + block)
+        total = total_ref[:, lanes] + product(2, 0, far_ref[bounds[2] : bounds[3], :, lanes])
         for row in range(tile_rows):
-            kind = 0 if row == 0 else 2 if row == tile_rows - 1 else 1
-            value = total[row * pitch : row * pitch + tile_cols]
-            value = value + bias_ref[kind : kind + 1, first : first + block]
+            bias = bias_ref[:, lanes] + shift_ref[1, :1, lanes]
+            over = shift_ref[0, :1, lanes]
+            under = shift_ref[2, :1, lanes]
+            bias = bias + (over * above if row == 0 else over)
+            bias = bias + (under * below if row == tile_rows - 1 else under)
+            value = total[row * pitch : row * pitch + tile_cols] + bias
             value = 0.5 * value * (1.0 + lax.erf(value * (0.5**0.5)))
-            out_ref[row, :, first : first + block] = value.astype(out_ref.dtype)
+            out_ref[row, :, lanes] = value.astype(out_ref.dtype)
 
 
 def one_stage(raw_fields, embed_weight, embed_bias, conv_weight, conv_bias):
@@ -160,59 +255,60 @@
             tile_rows=tile_rows,
             tile_breadth=tile_breadth,
         ),
-        out_shape=jax.ShapeDtypeStruct((devices, rows, PATCH, span), lowest),
+        out_shape=pltpu.VMEM((devices, rows, PATCH, span), lowest),
         name="windows",
     )(raw_fields)
     tile = lax.all_to_all(pieces, ("lat", "lon"), split_axis=0, concat_axis=0, tiled=True)
 
-    turned = embed_weight.transpose(2, 0, 1, 3).reshape(cells, channels)
-    bias_rows = jnp.broadcast_to(embed_bias, (8, channels))
-    taps = conv_weight.reshape(9, channels, channels)
-    weight, shift = pl.pallas_call(
+    whole = pl.BlockSpec(memory_space=pltpu.VMEM)
+    afar = pl.BlockSpec(memory_space=pl.ANY)
+    taps, near = 9, 2
+    close, far, shift = pl.pallas_call(
         compose_kernel,
-        grid=(9,),
-        in_specs=[
-            pl.BlockSpec((cells, channels), lambda t: (0, 0)),
-            pl.BlockSpec((8, channels), lambda t: (0, 0)),
-            pl.BlockSpec((1, channels, channels), lambda t: (t, 0, 0)),
+        in_specs=[whole, whole, afar],
+        out_specs=[whole, afar, whole],
+        out_shape=[
+            pltpu.VMEM((near, cells, channels), lowest),
+            jax.ShapeDtypeStruct((taps - near, cells, channels), lowest),
+            pltpu.VMEM((3, 8, channels), jnp.float32),
         ],
-        out_specs=[
-            pl.BlockSpec((1, cells, channels), lambda t: (t, 0, 0)),
-            pl.BlockSpec((1, 8, channels), lambda t: (t, 0, 0)),
+        scratch_shapes=[
+            pltpu.VMEM((channels // LANES, cells, LANES), jnp.float32),
+            pltpu.VMEM((cells + 16, channels), lowest),
+            pltpu.VMEM((taps, channels, channels), lowest),
+            pltpu.VMEM((taps - near, cells, channels), lowest),
+            pltpu.SemaphoreType.DMA((taps,)),
+            pltpu.SemaphoreType.DMA((taps - near,)),
         ],
-        out_shape=[
-            jax.ShapeDtypeStruct((9, cells, channels), lowest),
-            jax.ShapeDtypeStruct((9, 8, channels), jnp.float32),
-        ],
+        compiler_params=pltpu.CompilerParams(vmem_limit_bytes=48 << 20),
         name="compose",
-    )(turned, bias_rows, taps)
-    row_shift = shift[:, 0].reshape(3, 3, channels).sum(axis=1)
-    lat = lax.axis_index("lat")
-    above = jnp.where(lat > 0, 1.0, 0.0).astype(jnp.float32)
-    below = jnp.where(lat < lat_count - 1, 1.0, 0.0).astype(jnp.float32)
-    middle = conv_bias + row_shift[1]
-    both = middle + row_shift[0] + row_shift[2]
-    top = middle + above * row_shift[0] + row_shift[2]
-    bottom = middle + row_shift[0] + below * row_shift[2]
-    biases = jnp.stack([top, both, bottom])
-    edges = jnp.stack([above, below])
+    )(
+        pltpu.with_memory_space_constraint(embed_weight, pltpu.VMEM),
+        embed_bias.reshape(1, channels),
+        conv_weight.reshape(taps, channels, channels),
+    )
 
     return pl.pallas_call(
-        functools.partial(tokens_kernel, pitch=pitch, block=2 * LANES),
-        in_specs=[
-            pl.BlockSpec(memory_space=pltpu.SMEM),
-            pl.BlockSpec(memory_space=pltpu.VMEM),
-            pl.BlockSpec(memory_space=pltpu.VMEM),
-            pl.BlockSpec(memory_space=pltpu.VMEM),
-        ],
-        out_specs=pl.BlockSpec(memory_space=pltpu.VMEM),
+        functools.partial(tokens_kernel, pitch=pitch, block=4 * LANES),
+        in_specs=[whole, whole, afar, whole, whole],
+        out_specs=whole,
         out_shape=jax.ShapeDtypeStruct((tile_rows, tile_cols, channels), lowest),
         scratch_shapes=[
+            pltpu.VMEM((taps - near, cells, channels), lowest),
             pltpu.VMEM((rows, PATCH * pitch + 3 * PATCH, depth), jnp.float32),
             pltpu.VMEM((rows * pitch, 3 * cells), lowest),
+            pltpu.VMEM((tile_rows * pitch, channels), jnp.float32),
+            pltpu.SemaphoreType.DMA((3,)),
         ],
+        compiler_params=pltpu.CompilerParams(vmem_limit_bytes=32 << 20),
         name="tokens",
-    )(edges, tile, weight.reshape(9 * cells, channels), biases)
+    )(
+        pltpu.with_memory_space_constraint(tile, pltpu.VMEM),
+        pltpu.with_memory_space_constraint(close, pltpu.VMEM),
+        pltpu.with_memory_space_constraint(far, pltpu.HBM),
+        pltpu.with_memory_space_constraint(shift, pltpu.VMEM),
+        conv_bias.reshape(1, channels),
+    )
 
 
 def per_device(raw_fields, embed_weight, embed_bias, conv_weight, conv_bias):

time: 48 us -> 35.8 us (0.75)
  Pallas kernels: 32.8 us -> 24 us
  local copies, waits for them, and re-layouts: 6.1 us -> 1.91 us
  waiting for transfers between devices: 0.01 us -> 2.27 us
  other arithmetic: 1.31 us -> 0 us
    pallas_call x2, Pallas kernels: 30.7 us -> 21.9 us  [the longest x1 14.4 us: one_stage(): pl.pallas_call(compose_kernel, in_specs=[whole, whole, afar], out_specs=[...]
    all_to_all x1, waiting for transfers between devices: 0.01 us -> 2.27 us  [one_stage(): lax.all_to_all(pieces, ('lat', 'lon'), split_axis=0, concat_axis=0, tiled...]
    transpose x1 -> x0, local copies, waits for them, and re-layouts: 1.77 us -> none  [one_stage(): turned = embed_weight.transpose(2, 0, 1, 3).reshape(cells, channels)]
    broadcast_in_dim x1 -> x0, local copies, waits for them, and re-layouts: 1.29 us -> none  [one_stage(): bias_rows = jnp.broadcast_to(embed_bias, (8, channels))]
    another operation x2 -> x0, other arithmetic: 1.26 us -> none  [the longest x1 0.65 us: one_stage(): edges = jnp.stack([above, below])]
    reshape x1 -> x0, local copies, waits for them, and re-layouts: 1.11 us -> none  [one_stage(): turned = embed_weight.transpose(2, 0, 1, 3).reshape(cells, channels)]
    slice x2 -> x0, local copies, waits for them, and re-layouts: 1.06 us -> none  [the longest x1 1.05 us: one_stage(): row_shift = shift[:, 0].reshape(3, 3, channels).sum(axis=1)]
    unnamed x4 -> x6, local copies, waits for them, and re-layouts: 0.86 us -> 1.91 us
  transfers between devices with their start and end apart: 1 -> 1, of which waited for: 0 -> 1; matrix products, arithmetic and copies ran while one was open for 14% -> 0% of each run, Pallas kernels for 44% -> 41%
where the time goes in v2:
time: 35.8 us; the launch traced here: 35.5 us
  Pallas kernels  24 us (67%)
  starting transfers between devices  7.33 us (20%)
  waiting for transfers between devices  2.27 us (6%)
  local copies, waits for them, and re-layouts  1.91 us (5%)
    pallas_call x1, Pallas kernels, one_stage(): pl.pallas_call(compose_kernel, in_specs=[whole, whole, afar], out_specs=[...  14.4 us
    pallas_call x1, Pallas kernels, one_stage(): pl.pallas_call(functools.partial(tokens_kernel, pitch=pitch, block=4 * LA...  7.48 us
    all_to_all x1, starting transfers between devices, one_stage(): lax.all_to_all(pieces, ('lat', 'lon'), split_axis=0, concat_axis=0, tiled...  7.33 us
    all_to_all x1, waiting for transfers between devices, one_stage(): lax.all_to_all(pieces, ('lat', 'lon'), split_axis=0, concat_axis=0, tiled...  2.27 us
    pallas_call x1, Pallas kernels, one_stage(): pl.pallas_call(functools.partial(windows_kernel, lat_count=lat_count, lon...  2.15 us
    unnamed x6, local copies, waits for them, and re-layouts  1.91 us
  transfers between devices with their start and end apart: 1, of which 1 were waited for; matrix products, arithmetic and copies ran while one was open for 0% of the time, Pallas kernels for 41%

profile of v2, /device:TPU:0, one launch (start us, length us, event | category | flops | bytes accessed | tf_op | source)
XLA Modules:
  0.0 35.5 jit_solution(766937912671300628)
XLA Ops:
  0.0 2.2 %windows.1 = bf16[32,7,4,368]{3,2,1,0:T(4,128)(2,1)} custom-call(bf16[1,160,1440]{2,1,0:T(8,128)(2,1)} %raw_ref.1), custom_call_target="tpu_custom_call" | custom-call | tf_op jit(solution)/shard_map/windows/pallas_call | solution.py:250
  2.2 7.3 %all-to-all-start = ((bf16[32,7,4,368]{3,2,1,0:T(4,128)(2,1)}), bf16[32,7,4,368]{3,2,1,0:T(4,128)(2,1)S(1)}, u32[]{:S(2)}, u32[]{:S(2)}) async-start(bf16[32,7,4,368]{3,2,1,0:T(4,128)(2,1)} %windows.1), calls=%async_computation | async-start | bytes 1376256 | tf_op jit(solution)/shard_map/all_to_all | solution.py:261
  9.5 0.0 copy-start
  9.5 1.2 %copy-done = bf16[32,4,4,1024]{3,2,1,0:T(4,128)(2,1)S(1)} copy-done((bf16[32,4,4,1024]{3,2,1,0:T(4,128)(2,1)S(1)}, bf16[32,4,4,1024]{3,2,1,0:T(4,128)(2,1)}, u32[]{:S(2)}) %copy-start) | copy-done | bytes 1048600
  10.7 0.0 copy-start.2
  10.7 0.7 %copy-done.2 = f32[1024]{0:T(1024)S(1)} copy-done((f32[1024]{0:T(1024)S(1)}, f32[1024]{0:T(1024)}, u32[]{:S(2)}) %copy-start.2) | copy-done | bytes 4120
  11.4 0.0 copy-start.1
  11.4 14.4 %compose.1 = (bf16[2,512,1024]{2,1,0:T(8,128)(2,1)S(1)}, bf16[7,512,1024]{2,1,0:T(8,128)(2,1)}, f32[3,8,1024]{2,1,0:T(8,128)S(1)}) custom-call(bf16[32,4,4,1024]{3,2,1,0:T(4,128)(2,1)S(1)} %copy-done, f32[1,1024]{1,0:T(1,128)S(1)} %bitcast.4, bf16[9,1024,1024]{2,1,0:T(8,128)(2,1)} %bitcast.5), custom_call_target="tpu_custom_call" | custom-call | tf_op jit(solution)/shard_map/compose/pallas_call | solution.py:266
  25.8 2.3 %all-to-all-done.tile_ref = bf16[32,7,4,368]{3,2,1,0:T(4,128)(2,1)S(1)} async-done(((bf16[32,7,4,368]{3,2,1,0:T(4,128)(2,1)}), bf16[32,7,4,368]{3,2,1,0:T(4,128)(2,1)S(1)}, u32[]{:S(2)}, u32[]{:S(2)}) %all-to-all-start) | async-done | bytes 659488 | tf_op jit(solution)/shard_map/all_to_all | solution.py:261
  28.1 0.0 copy-done.1
  28.1 7.5 %tokens.1 = bf16[5,90,1024]{2,1,0:T(8,128)(2,1)} custom-call(bf16[32,7,4,368]{3,2,1,0:T(4,128)(2,1)S(1)} %all-to-all-done.tile_ref, bf16[2,512,1024]{2,1,0:T(8,128)(2,1)S(1)} %get-tuple-element.8.near_ref, bf16[7,512,1024]{2,1,0:T(8,128)(2,1)} %get-tuple-element.9.far_hbm, f32[3,8,1024]{2,1,0:T(8,128)S(1)} %get-tuple-element.10.shift_ref, f32[1,1024]{1,0:T(1,128)S(1)} %bitcast.3), custom_call_target="tpu_custom_call" | custom-call | tf_op jit(solution)/shard_map/tokens/pallas_call | solution.py:291
Async XLA Ops:
  2.2 25.9 %all-to-all-start = ((bf16[32,7,4,368]{3,2,1,0:T(4,128)(2,1)}), bf16[32,7,4,368]{3,2,1,0:T(4,128)(2,1)S(1)}, u32[]{:S(2)}, u32[]{:S(2)}) async-start(bf16[32,7,4,368]{3,2,1,0:T(4,128)(2,1)} %windows.1), calls=%async_computation | async-start | bytes 1376256 | tf_op jit(solution)/shard_map/all_to_all | solution.py:261
  9.5 1.2 %copy-start = (bf16[32,4,4,1024]{3,2,1,0:T(4,128)(2,1)S(1)}, bf16[32,4,4,1024]{3,2,1,0:T(4,128)(2,1)}, u32[]{:S(2)}) copy-start(bf16[32,4,4,1024]{3,2,1,0:T(4,128)(2,1)} %embed_ref.1) | copy-start | bytes 3145732
  10.7 0.7 %copy-start.2 = (f32[1024]{0:T(1024)S(1)}, f32[1024]{0:T(1024)}, u32[]{:S(2)}) copy-start(f32[1024]{0:T(1024)} %param.7) | copy-start | bytes 12292
  11.4 16.7 %copy-start.1 = (f32[1024]{0:T(1024)S(1)}, f32[1024]{0:T(1024)}, u32[]{:S(2)}) copy-start(f32[1024]{0:T(1024)} %param.9) | copy-start | bytes 12292

commit v3 on v2

--- a/solution.py
+++ b/solution.py
@@ -85,10 +85,13 @@
 
 def compose_kernel(
     embed_ref,
-    bias_ref,
+    embed_bias_ref,
+    conv_bias_ref,
     conv_hbm,
     near_ref,
     far_hbm,
+    bias_ref,
+    edge_ref,
     shift_ref,
     plain_ref,
     left_ref,
@@ -111,7 +114,7 @@
 
     for tap in range(taps):
         fetch(tap).start()
-    rest = bias_ref[...]
+    rest = embed_bias_ref[...]
     lines = lax.broadcasted_iota(jnp.int32, (rim, rest.shape[1]), 0)
     below = jnp.zeros(lines.shape, jnp.float32)
     for line in range(3):
@@ -153,6 +156,16 @@
 
     lax.fori_loop(0, near, compose_near, None)
     lax.fori_loop(0, taps - near, compose_far, None)
+    lat = lax.axis_index("lat")
+    above = jnp.where(lat > 0, 1.0, 0.0).astype(jnp.float32)
+    below = jnp.where(lat < lax.axis_size("lat") - 1, 1.0, 0.0).astype(jnp.float32)
+    edge_ref[0] = jnp.full(edge_ref.shape[1:], above)
+    edge_ref[1] = jnp.full(edge_ref.shape[1:], below)
+    middle = conv_bias_ref[...] + shift_ref[1]
+    over, under = shift_ref[0], shift_ref[2]
+    bias_ref[0] = middle + over * above + under
+    bias_ref[1] = middle + over + under
+    bias_ref[2] = middle + over + under * below
     for tap in range(taps - near):
         send(tap).wait()
 
@@ -161,14 +174,16 @@
     tile_ref,
     near_ref,
     far_hbm,
-    shift_ref,
     bias_ref,
-    out_ref,
+    edge_ref,
+    out_hbm,
     far_ref,
     turned_ref,
     cells_ref,
     total_ref,
+    out_ref,
     arrived,
+    left,
     *,
     pitch,
     block,
@@ -179,31 +194,36 @@
     cells = depth * PATCH
     steps = 3 * PATCH
     near = near_ref.shape[0]
-    bounds = (0, 3 - near, 6 - near, 9 - near)
-
-    def fetch(tap_row):
-        taps = pl.ds(bounds[tap_row], bounds[tap_row + 1] - bounds[tap_row])
-        return pltpu.make_async_copy(far_hbm.at[taps], far_ref.at[taps], arrived.at[tap_row])
-
-    for tap_row in range(3):
-        fetch(tap_row).start()
-    lat = lax.axis_index("lat")
-    above = jnp.where(lat > 0, 1.0, 0.0).astype(jnp.float32)
-    below = jnp.where(lat < lax.axis_size("lat") - 1, 1.0, 0.0).astype(jnp.float32)
+    groups = ((near, 3), (3, 4), (4, 6), (6, 9))
+
+    def fetch(group):
+        start, stop = groups[group]
+        taps = pl.ds(start - near, stop - start)
+        return pltpu.make_async_copy(far_hbm.at[taps], far_ref.at[taps], arrived.at[group])
+
+    def send(part):
+        lanes = slice(part * block, (part + 1) * block)
+        return pltpu.make_async_copy(
+            out_ref.at[:, :, lanes], out_hbm.at[:, :, lanes], left.at[part]
+        )
+
+    for group in range(len(groups)):
+        fetch(group).start()
     for row in range(rows):
-        tile = tile_ref[:, row].astype(jnp.float32).reshape(depth, span)
+        turned = tile_ref[:, row].astype(jnp.float32).reshape(depth, span).T
         if row == 0:
-            tile = tile * above
+            turned = turned * edge_ref[0, :1]
         if row == rows - 1:
-            tile = tile * below
-        turned_ref[row, :span] = tile.T
+            turned = turned * edge_ref[1, :1]
+        turned_ref[row, :span] = turned
         for step in range(steps):
             picked = turned_ref[row, pl.ds(step, pitch, stride=PATCH), :]
             cells_ref[row * pitch : (row + 1) * pitch, step * depth : (step + 1) * depth] = (
                 picked.astype(cells_ref.dtype)
             )
 
-    def product(tap_row, first, weight):
+    def product(start, weight):
+        tap_row, first = divmod(start, 3)
         count = weight.shape[0]
         left = cells_ref[
             tap_row * pitch : (tap_row + tile_rows) * pitch, first * cells : (first + count) * cells
@@ -211,24 +231,22 @@
         right = weight.reshape(count * cells, weight.shape[2])
         return jnp.dot(left, right, preferred_element_type=jnp.float32)
 
-    total_ref[...] = product(0, 0, near_ref[...])
-    fetch(0).wait()
-    total_ref[...] += product(0, near, far_ref[bounds[0] : bounds[1]])
-    fetch(1).wait()
-    total_ref[...] += product(1, 0, far_ref[bounds[1] : bounds[2]])
-    fetch(2).wait()
-    for first in range(0, channels, block):
-        lanes = slice(first, first + block)
-        total = total_ref[:, lanes] + product(2, 0, far_ref[bounds[2] : bounds[3], :, lanes])
+    total_ref[...] = product(0, near_ref[...])
+    for group, (start, stop) in enumerate(groups):
+        fetch(group).wait()
+        if stop < 9:
+            total_ref[...] += product(start, far_ref[start - near : stop - near])
+    for part in range(channels // block):
+        lanes = slice(part * block, (part + 1) * block)
+        total = total_ref[:, lanes] + product(start, far_ref[start - near : stop - near, :, lanes])
         for row in range(tile_rows):
-            bias = bias_ref[:, lanes] + shift_ref[1, :1, lanes]
-            over = shift_ref[0, :1, lanes]
-            under = shift_ref[2, :1, lanes]
-            bias = bias + (over * above if row == 0 else over)
-            bias = bias + (under * below if row == tile_rows - 1 else under)
-            value = total[row * pitch : row * pitch + tile_cols] + bias
+            kind = 0 if row == 0 else 2 if row == tile_rows - 1 else 1
+            value = total[row * pitch : row * pitch + tile_cols] + bias_ref[kind, :1, lanes]
             value = 0.5 * value * (1.0 + lax.erf(value * (0.5**0.5)))
             out_ref[row, :, lanes] = value.astype(out_ref.dtype)
+        send(part).start()
+    for part in range(channels // block):
+        send(part).wait()
 
 
 def one_stage(raw_fields, embed_weight, embed_bias, conv_weight, conv_bias):
@@ -263,16 +281,19 @@
     whole = pl.BlockSpec(memory_space=pltpu.VMEM)
     afar = pl.BlockSpec(memory_space=pl.ANY)
     taps, near = 9, 2
-    close, far, shift = pl.pallas_call(
+    block = channels // 2
+    close, far, bias, edge = pl.pallas_call(
         compose_kernel,
-        in_specs=[whole, whole, afar],
-        out_specs=[whole, afar, whole],
+        in_specs=[whole, whole, whole, afar],
+        out_specs=[whole, afar, whole, whole],
         out_shape=[
             pltpu.VMEM((near, cells, channels), lowest),
             jax.ShapeDtypeStruct((taps - near, cells, channels), lowest),
             pltpu.VMEM((3, 8, channels), jnp.float32),
+            pltpu.VMEM((2, 8, depth), jnp.float32),
         ],
         scratch_shapes=[
+            pltpu.VMEM((3, 8, channels), jnp.float32),
             pltpu.VMEM((channels // LANES, cells, LANES), jnp.float32),
             pltpu.VMEM((cells + 16, channels), lowest),
             pltpu.VMEM((taps, channels, channels), lowest),
@@ -285,20 +306,23 @@
     )(
         pltpu.with_memory_space_constraint(embed_weight, pltpu.VMEM),
         embed_bias.reshape(1, channels),
+        conv_bias.reshape(1, channels),
         conv_weight.reshape(taps, channels, channels),
     )
 
     return pl.pallas_call(
-        functools.partial(tokens_kernel, pitch=pitch, block=4 * LANES),
+        functools.partial(tokens_kernel, pitch=pitch, block=block),
         in_specs=[whole, whole, afar, whole, whole],
-        out_specs=whole,
+        out_specs=afar,
         out_shape=jax.ShapeDtypeStruct((tile_rows, tile_cols, channels), lowest),
         scratch_shapes=[
             pltpu.VMEM((taps - near, cells, channels), lowest),
             pltpu.VMEM((rows, PATCH * pitch + 3 * PATCH, depth), jnp.float32),
             pltpu.VMEM((rows * pitch, 3 * cells), lowest),
             pltpu.VMEM((tile_rows * pitch, channels), jnp.float32),
-            pltpu.SemaphoreType.DMA((3,)),
+            pltpu.VMEM((tile_rows, tile_cols, channels), lowest),
+            pltpu.SemaphoreType.DMA((4,)),
+            pltpu.SemaphoreType.DMA((channels // block,)),
         ],
         compiler_params=pltpu.CompilerParams(vmem_limit_bytes=32 << 20),
         name="tokens",
@@ -306,14 +330,16 @@
         pltpu.with_memory_space_constraint(tile, pltpu.VMEM),
         pltpu.with_memory_space_constraint(close, pltpu.VMEM),
         pltpu.with_memory_space_constraint(far, pltpu.HBM),
-        pltpu.with_memory_space_constraint(shift, pltpu.VMEM),
-        conv_bias.reshape(1, channels),
+        pltpu.with_memory_space_constraint(bias, pltpu.VMEM),
+        pltpu.with_memory_space_constraint(edge, pltpu.VMEM),
     )
 
 
 def per_device(raw_fields, embed_weight, embed_bias, conv_weight, conv_bias):
     variables, _, _, channels = embed_weight.shape
-    if raw_fields.shape[0] == 1 and variables * PATCH * PATCH <= channels:
+    tile_height = raw_fields.shape[1] // lax.axis_size("lat")
+    deep = variables * PATCH * PATCH > channels
+    if raw_fields.shape[0] == 1 and tile_height >= 2 * PATCH and not deep:
         return one_stage(raw_fields, embed_weight, embed_bias, conv_weight, conv_bias)
     return two_stages(raw_fields, embed_weight, embed_bias, conv_weight, conv_bias)
 

time: 35.8 us -> 34.7 us (0.969)
  Pallas kernels: 24 us -> 22.8 us
  local copies, waits for them, and re-layouts: 1.91 us -> 2.59 us
  waiting for transfers between devices: 2.27 us -> 1.6 us
    pallas_call x2, Pallas kernels: 21.9 us -> 20.7 us  [the longest x1 14.4 us: one_stage(): pl.pallas_call(compose_kernel, in_specs=[whole, whole, whole, afar], out_...]
    unnamed x6, local copies, waits for them, and re-layouts: 1.91 us -> 2.59 us
    all_to_all x1, waiting for transfers between devices: 2.27 us -> 1.6 us  [one_stage(): lax.all_to_all(pieces, ('lat', 'lon'), split_axis=0, concat_axis=0, tiled...]
  transfers between devices with their start and end apart: 1 -> 1, of which waited for: 1 -> 1; matrix products, arithmetic and copies ran while one was open for 0% -> 0% of each run, Pallas kernels for 41% -> 42%
where the time goes in v3:
time: 34.7 us; the launch traced here: 34.4 us
  Pallas kernels  22.8 us (66%)
  starting transfers between devices  7.33 us (21%)
  local copies, waits for them, and re-layouts  2.59 us (7%)
  waiting for transfers between devices  1.6 us (5%)
    pallas_call x1, Pallas kernels, one_stage(): pl.pallas_call(compose_kernel, in_specs=[whole, whole, whole, afar], out_...  14.4 us
    all_to_all x1, starting transfers between devices, one_stage(): lax.all_to_all(pieces, ('lat', 'lon'), split_axis=0, concat_axis=0, tiled...  7.33 us
    pallas_call x1, Pallas kernels, one_stage(): pl.pallas_call(functools.partial(tokens_kernel, pitch=pitch, block=block)...  6.31 us
    unnamed x6, local copies, waits for them, and re-layouts  2.59 us
    pallas_call x1, Pallas kernels, one_stage(): pl.pallas_call(functools.partial(windows_kernel, lat_count=lat_count, lon...  2.15 us
    all_to_all x1, waiting for transfers between devices, one_stage(): lax.all_to_all(pieces, ('lat', 'lon'), split_axis=0, concat_axis=0, tiled...  1.6 us
  transfers between devices with their start and end apart: 1, of which 1 were waited for; matrix products, arithmetic and copies ran while one was open for 0% of the time, Pallas kernels for 42%

profile of v3, /device:TPU:0, one launch (start us, length us, event | category | flops | bytes accessed | tf_op | source)
XLA Modules:
  0.0 34.4 jit_solution(17376985875960843811)
XLA Ops:
  0.0 2.2 %windows.1 = bf16[32,7,4,368]{3,2,1,0:T(4,128)(2,1)} custom-call(bf16[1,160,1440]{2,1,0:T(8,128)(2,1)} %raw_ref.1), custom_call_target="tpu_custom_call" | custom-call | tf_op jit(solution)/shard_map/windows/pallas_call | solution.py:268
  2.2 7.3 %all-to-all-start = ((bf16[32,7,4,368]{3,2,1,0:T(4,128)(2,1)}), bf16[32,7,4,368]{3,2,1,0:T(4,128)(2,1)S(1)}, u32[]{:S(2)}, u32[]{:S(2)}) async-start(bf16[32,7,4,368]{3,2,1,0:T(4,128)(2,1)} %windows.1), calls=%async_computation | async-start | bytes 1376256 | tf_op jit(solution)/shard_map/all_to_all | solution.py:279
  9.5 0.0 copy-start
  9.5 1.2 %copy-done = bf16[32,4,4,1024]{3,2,1,0:T(4,128)(2,1)S(1)} copy-done((bf16[32,4,4,1024]{3,2,1,0:T(4,128)(2,1)S(1)}, bf16[32,4,4,1024]{3,2,1,0:T(4,128)(2,1)}, u32[]{:S(2)}) %copy-start) | copy-done | bytes 1048600
  10.7 0.0 copy-start.1
  10.7 0.7 %copy-done.1 = f32[1024]{0:T(1024)S(1)} copy-done((f32[1024]{0:T(1024)S(1)}, f32[1024]{0:T(1024)}, u32[]{:S(2)}) %copy-start.1) | copy-done | bytes 4120
  11.4 0.0 copy-start.2
  11.4 0.7 %copy-done.2 = f32[1024]{0:T(1024)S(1)} copy-done((f32[1024]{0:T(1024)S(1)}, f32[1024]{0:T(1024)}, u32[]{:S(2)}) %copy-start.2) | copy-done | bytes 4120
  12.1 14.4 %compose.1 = (bf16[2,512,1024]{2,1,0:T(8,128)(2,1)S(1)}, bf16[7,512,1024]{2,1,0:T(8,128)(2,1)}, f32[3,8,1024]{2,1,0:T(8,128)S(1)}, f32[2,8,128]{2,1,0:T(8,128)S(1)}) custom-call(bf16[32,4,4,1024]{3,2,1,0:T(4,128)(2,1)S(1)} %copy-done, f32[1,1024]{1,0:T(1,128)S(1)} %bitcast.3, f32[1,1024]{1,0:T(1,128)S(1)} %bitcast.4, bf16[9,1024,1024]{2,1,0:T(8,128)(2,1)} %bitcast.5), custom_call_target="tpu_custom_call" | custom-call | tf_op jit(solution)/shard_map/compose/pallas_call | solution.py:285
  26.5 1.6 %all-to-all-done.tile_ref = bf16[32,7,4,368]{3,2,1,0:T(4,128)(2,1)S(1)} async-done(((bf16[32,7,4,368]{3,2,1,0:T(4,128)(2,1)}), bf16[32,7,4,368]{3,2,1,0:T(4,128)(2,1)S(1)}, u32[]{:S(2)}, u32[]{:S(2)}) %all-to-all-start) | async-done | bytes 659488 | tf_op jit(solution)/shard_map/all_to_all | solution.py:279
  28.1 6.3 %tokens.1 = bf16[5,90,1024]{2,1,0:T(8,128)(2,1)} custom-call(bf16[32,7,4,368]{3,2,1,0:T(4,128)(2,1)S(1)} %all-to-all-done.tile_ref, bf16[2,512,1024]{2,1,0:T(8,128)(2,1)S(1)} %get-tuple-element.9.near_ref, bf16[7,512,1024]{2,1,0:T(8,128)(2,1)} %get-tuple-element.10.far_hbm, f32[3,8,1024]{2,1,0:T(8,128)S(1)} %get-tuple-element.11.bias_ref, ...), custom_call_target="tpu_custom_call" | custom-call | tf_op jit(solution)/shard_map/tokens/pallas_call | solution.py:313
Async XLA Ops:
  2.2 25.9 %all-to-all-start = ((bf16[32,7,4,368]{3,2,1,0:T(4,128)(2,1)}), bf16[32,7,4,368]{3,2,1,0:T(4,128)(2,1)S(1)}, u32[]{:S(2)}, u32[]{:S(2)}) async-start(bf16[32,7,4,368]{3,2,1,0:T(4,128)(2,1)} %windows.1), calls=%async_computation | async-start | bytes 1376256 | tf_op jit(solution)/shard_map/all_to_all | solution.py:279
  9.5 1.2 %copy-start = (bf16[32,4,4,1024]{3,2,1,0:T(4,128)(2,1)S(1)}, bf16[32,4,4,1024]{3,2,1,0:T(4,128)(2,1)}, u32[]{:S(2)}) copy-start(bf16[32,4,4,1024]{3,2,1,0:T(4,128)(2,1)} %embed_ref.1) | copy-start | bytes 3145732
  10.7 0.7 %copy-start.1 = (f32[1024]{0:T(1024)S(1)}, f32[1024]{0:T(1024)}, u32[]{:S(2)}) copy-start(f32[1024]{0:T(1024)} %param.7) | copy-start | bytes 12292
  11.4 0.7 %copy-start.2 = (f32[1024]{0:T(1024)S(1)}, f32[1024]{0:T(1024)}, u32[]{:S(2)}) copy-start(f32[1024]{0:T(1024)} %param.9) | copy-start | bytes 12292

commit v4 on v3

--- a/solution.py
+++ b/solution.py
@@ -84,19 +84,23 @@
 
 
 def compose_kernel(
-    embed_ref,
-    embed_bias_ref,
-    conv_bias_ref,
+    embed_hbm,
+    embed_bias_hbm,
+    conv_bias_hbm,
     conv_hbm,
     near_ref,
     far_hbm,
     bias_ref,
     edge_ref,
+    embed_ref,
+    embed_bias_ref,
+    conv_bias_ref,
     shift_ref,
     plain_ref,
     left_ref,
     taps_ref,
     made_ref,
+    came,
     arrived,
     left,
 ):
@@ -112,8 +116,22 @@
     def send(tap):
         return pltpu.make_async_copy(made_ref.at[tap], far_hbm.at[tap], left.at[tap])
 
+    small = [
+        pltpu.make_async_copy(source, target, came.at[place])
+        for place, (source, target) in enumerate(
+            (
+                (embed_bias_hbm, embed_bias_ref),
+                (conv_bias_hbm, conv_bias_ref),
+                (embed_hbm, embed_ref),
+            )
+        )
+    ]
+    for copy in small:
+        copy.start()
     for tap in range(taps):
-        fetch(tap).start()
+        fetch(tap).start(priority=1)
+    for copy in small:
+        copy.wait()
     rest = embed_bias_ref[...]
     lines = lax.broadcasted_iota(jnp.int32, (rim, rest.shape[1]), 0)
     below = jnp.zeros(lines.shape, jnp.float32)
@@ -284,7 +302,7 @@
     block = channels // 2
     close, far, bias, edge = pl.pallas_call(
         compose_kernel,
-        in_specs=[whole, whole, whole, afar],
+        in_specs=[afar] * 4,
         out_specs=[whole, afar, whole, whole],
         out_shape=[
             pltpu.VMEM((near, cells, channels), lowest),
@@ -293,21 +311,30 @@
             pltpu.VMEM((2, 8, depth), jnp.float32),
         ],
         scratch_shapes=[
+            pltpu.VMEM(embed_weight.shape, lowest),
+            pltpu.VMEM((1, channels), jnp.float32),
+            pltpu.VMEM((1, channels), jnp.float32),
             pltpu.VMEM((3, 8, channels), jnp.float32),
             pltpu.VMEM((channels // LANES, cells, LANES), jnp.float32),
             pltpu.VMEM((cells + 16, channels), lowest),
             pltpu.VMEM((taps, channels, channels), lowest),
             pltpu.VMEM((taps - near, cells, channels), lowest),
+            pltpu.SemaphoreType.DMA((3,)),
             pltpu.SemaphoreType.DMA((taps,)),
             pltpu.SemaphoreType.DMA((taps - near,)),
         ],
         compiler_params=pltpu.CompilerParams(vmem_limit_bytes=48 << 20),
         name="compose",
     )(
-        pltpu.with_memory_space_constraint(embed_weight, pltpu.VMEM),
-        embed_bias.reshape(1, channels),
-        conv_bias.reshape(1, channels),
-        conv_weight.reshape(taps, channels, channels),
+        *(
+            pltpu.with_memory_space_constraint(value, pltpu.HBM)
+            for value in (
+                embed_weight,
+                embed_bias.reshape(1, channels),
+                conv_bias.reshape(1, channels),
+                conv_weight.reshape(taps, channels, channels),
+            )
+        )
     )
 
     return pl.pallas_call(

time: 34.7 us -> 34.6 us (level)
  local copies, waits for them, and re-layouts: 2.59 us -> 0 us
  waiting for transfers between devices: 1.6 us -> 3.45 us
  Pallas kernels: 22.8 us -> 23.6 us
    unnamed x6 -> x0, local copies, waits for them, and re-layouts: 2.59 us -> none
    all_to_all x1, waiting for transfers between devices: 1.6 us -> 3.45 us  [one_stage(): lax.all_to_all(pieces, ('lat', 'lon'), split_axis=0, concat_axis=0, tiled...]
    pallas_call x1, Pallas kernels: 14.4 us -> 15.1 us  [one_stage(): pl.pallas_call(compose_kernel, in_specs=[afar] * 4, out_specs=[whole, afa...]
  transfers between devices with their start and end apart: 1 -> 1, of which waited for: 1 -> 1; matrix products, arithmetic and copies ran while one was open for 0% -> 0% of each run, Pallas kernels for 42% -> 44%
where the time goes in v4:
time: 34.6 us; the launch traced here: 34.4 us
  Pallas kernels  23.6 us (68%)
  starting transfers between devices  7.33 us (21%)
  waiting for transfers between devices  3.45 us (10%)
    pallas_call x1, Pallas kernels, one_stage(): pl.pallas_call(compose_kernel, in_specs=[afar] * 4, out_specs=[whole, afa...  15.1 us
    all_to_all x1, starting transfers between devices, one_stage(): lax.all_to_all(pieces, ('lat', 'lon'), split_axis=0, concat_axis=0, tiled...  7.33 us
    pallas_call x1, Pallas kernels, one_stage(): pl.pallas_call(functools.partial(tokens_kernel, pitch=pitch, block=block)...  6.31 us
    all_to_all x1, waiting for transfers between devices, one_stage(): lax.all_to_all(pieces, ('lat', 'lon'), split_axis=0, concat_axis=0, tiled...  3.45 us
    pallas_call x1, Pallas kernels, one_stage(): pl.pallas_call(functools.partial(windows_kernel, lat_count=lat_count, lon...  2.15 us
  transfers between devices with their start and end apart: 1, of which 1 were waited for; matrix products, arithmetic and copies ran while one was open for 0% of the time, Pallas kernels for 44%

profile of v4, /device:TPU:0, one launch (start us, length us, event | category | flops | bytes accessed | tf_op | source)
XLA Modules:
  0.0 34.4 jit_solution(11964387337785613944)
XLA Ops:
  0.0 2.2 %windows.1 = bf16[32,7,4,368]{3,2,1,0:T(4,128)(2,1)} custom-call(bf16[1,160,1440]{2,1,0:T(8,128)(2,1)} %raw_ref.1), custom_call_target="tpu_custom_call" | custom-call | tf_op jit(solution)/shard_map/windows/pallas_call | solution.py:286
  2.2 7.3 %all-to-all-start = ((bf16[32,7,4,368]{3,2,1,0:T(4,128)(2,1)}), bf16[32,7,4,368]{3,2,1,0:T(4,128)(2,1)S(1)}, u32[]{:S(2)}, u32[]{:S(2)}) async-start(bf16[32,7,4,368]{3,2,1,0:T(4,128)(2,1)} %windows.1), calls=%async_computation | async-start | bytes 1376256 | tf_op jit(solution)/shard_map/all_to_all | solution.py:297
  9.5 15.1 %compose.1 = (bf16[2,512,1024]{2,1,0:T(8,128)(2,1)S(1)}, bf16[7,512,1024]{2,1,0:T(8,128)(2,1)}, f32[3,8,1024]{2,1,0:T(8,128)S(1)}, f32[2,8,128]{2,1,0:T(8,128)S(1)}) custom-call(bf16[32,4,4,1024]{3,2,1,0:T(4,128)(2,1)} %embed_hbm.1, f32[1,1024]{1,0:T(1,128)} %bitcast.4, f32[1,1024]{1,0:T(1,128)} %bitcast.5, bf16[9,1024,1024]{2,1,0:T(8,128)(2,1)} %bitcast.3), custom_call_target="tpu_custom_call" | custom-call | tf_op jit(solution)/shard_map/compose/pallas_call | solution.py:303
  24.6 3.4 %all-to-all-done.tile_ref = bf16[32,7,4,368]{3,2,1,0:T(4,128)(2,1)S(1)} async-done(((bf16[32,7,4,368]{3,2,1,0:T(4,128)(2,1)}), bf16[32,7,4,368]{3,2,1,0:T(4,128)(2,1)S(1)}, u32[]{:S(2)}, u32[]{:S(2)}) %all-to-all-start) | async-done | bytes 659488 | tf_op jit(solution)/shard_map/all_to_all | solution.py:297
  28.1 6.3 %tokens.1 = bf16[5,90,1024]{2,1,0:T(8,128)(2,1)} custom-call(bf16[32,7,4,368]{3,2,1,0:T(4,128)(2,1)S(1)} %all-to-all-done.tile_ref, bf16[2,512,1024]{2,1,0:T(8,128)(2,1)S(1)} %get-tuple-element.9.near_ref, bf16[7,512,1024]{2,1,0:T(8,128)(2,1)} %get-tuple-element.10.far_hbm, f32[3,8,1024]{2,1,0:T(8,128)S(1)} %get-tuple-element.11.bias_ref, ...), custom_call_target="tpu_custom_call" | custom-call | tf_op jit(solution)/shard_map/tokens/pallas_call | solution.py:340
Async XLA Ops:
  2.2 25.9 %all-to-all-start = ((bf16[32,7,4,368]{3,2,1,0:T(4,128)(2,1)}), bf16[32,7,4,368]{3,2,1,0:T(4,128)(2,1)S(1)}, u32[]{:S(2)}, u32[]{:S(2)}) async-start(bf16[32,7,4,368]{3,2,1,0:T(4,128)(2,1)} %windows.1), calls=%async_computation | async-start | bytes 1376256 | tf_op jit(solution)/shard_map/all_to_all | solution.py:297

commit v5 on v4

--- a/solution.py
+++ b/solution.py
@@ -59,28 +59,53 @@
     return result.reshape(patch_rows, patch_cols, channels)
 
 
-def windows_kernel(raw_ref, out_ref, *, lat_count, lon_count, tile_rows, tile_breadth):
-    height, breadth = raw_ref.shape[1:]
-    span = tile_breadth + 2 * PATCH
+def windows_kernel(
+    raw_hbm, out_hbm, raw_ref, out_ref, arrived, left, *, lat_count, lon_count, tile_rows
+):
+    height, breadth = raw_ref.shape
+    _, rows, _, span = out_ref.shape
+    tile_breadth = breadth // lon_count
     patches_high = height // PATCH
-    rows = tile_rows + 2
-    raw = raw_ref[0]
-    for lon in range(lon_count):
-        first = lon * tile_breadth - PATCH
-        last = first + span
-        if first < 0:
-            window = jnp.concatenate([raw[:, first:], raw[:, :last]], axis=1)
-        elif last > breadth:
-            window = jnp.concatenate([raw[:, first:], raw[:, : last - breadth]], axis=1)
-        else:
-            window = raw[:, first:last]
-        for patch_row in range(patches_high):
-            piece = window[PATCH * patch_row : PATCH * (patch_row + 1)]
+    pieces = arrived.shape[0]
+    share = height // pieces
+
+    def fetch(piece):
+        lines = pl.ds(piece * share, share)
+        return pltpu.make_async_copy(raw_hbm.at[0, lines], raw_ref.at[lines], arrived.at[piece])
+
+    def send(lat):
+        tiles = pl.ds(lat * lon_count, lon_count)
+        return pltpu.make_async_copy(out_ref.at[tiles], out_hbm.at[tiles], left.at[lat])
+
+    def wanted(lat, step):
+        return min(max(lat * tile_rows - 1 + step, 0), patches_high - 1)
+
+    for piece in range(pieces):
+        fetch(piece).start()
+    for piece in range(pieces):
+        fetch(piece).wait()
+        raw = raw_ref[piece * share : (piece + 1) * share]
+        low, high = piece * share // PATCH, (piece + 1) * share // PATCH
+        for lon in range(lon_count):
+            first = lon * tile_breadth - PATCH
+            last = first + span
+            if first < 0:
+                window = jnp.concatenate([raw[:, first:], raw[:, :last]], axis=1)
+            elif last > breadth:
+                window = jnp.concatenate([raw[:, first:], raw[:, : last - breadth]], axis=1)
+            else:
+                window = raw[:, first:last]
             for lat in range(lat_count):
                 for step in range(rows):
-                    wanted = lat * tile_rows - 1 + step
-                    if min(max(wanted, 0), patches_high - 1) == patch_row:
-                        out_ref[lat * lon_count + lon, step] = piece
+                    row = wanted(lat, step)
+                    if low <= row < high:
+                        start = PATCH * (row - low)
+                        out_ref[lat * lon_count + lon, step] = window[start : start + PATCH]
+        for lat in range(lat_count):
+            if low <= wanted(lat, rows - 1) < high:
+                send(lat).start()
+    for lat in range(lat_count):
+        send(lat).wait()
 
 
 def compose_kernel(
@@ -283,17 +308,22 @@
     pitch = -(-(tile_cols + 2) // 16) * 16
     lowest = jnp.bfloat16
 
+    halves = 2 if height % (4 * PATCH) == 0 else 1
     pieces = pl.pallas_call(
         functools.partial(
-            windows_kernel,
-            lat_count=lat_count,
-            lon_count=lon_count,
-            tile_rows=tile_rows,
-            tile_breadth=tile_breadth,
+            windows_kernel, lat_count=lat_count, lon_count=lon_count, tile_rows=tile_rows
         ),
-        out_shape=pltpu.VMEM((devices, rows, PATCH, span), lowest),
+        in_specs=[pl.BlockSpec(memory_space=pl.ANY)],
+        out_specs=pl.BlockSpec(memory_space=pl.ANY),
+        out_shape=jax.ShapeDtypeStruct((devices, rows, PATCH, span), lowest),
+        scratch_shapes=[
+            pltpu.VMEM((height, breadth), lowest),
+            pltpu.VMEM((devices, rows, PATCH, span), lowest),
+            pltpu.SemaphoreType.DMA((halves,)),
+            pltpu.SemaphoreType.DMA((lat_count,)),
+        ],
         name="windows",
-    )(raw_fields)
+    )(pltpu.with_memory_space_constraint(raw_fields, pltpu.HBM))
     tile = lax.all_to_all(pieces, ("lat", "lon"), split_axis=0, concat_axis=0, tiled=True)
 
     whole = pl.BlockSpec(memory_space=pltpu.VMEM)

time: 34.6 us -> 34.6 us (level)
  no operation moved by 1% of the time
where the time goes in v5:
time: 34.6 us; the launch traced here: 34.4 us
  Pallas kernels  23.6 us (68%)
  starting transfers between devices  7.33 us (21%)
  waiting for transfers between devices  3.43 us (10%)
    pallas_call x1, Pallas kernels, one_stage(): pl.pallas_call(compose_kernel, in_specs=[afar] * 4, out_specs=[whole, afa...  15.1 us
    all_to_all x1, starting transfers between devices, one_stage(): lax.all_to_all(pieces, ('lat', 'lon'), split_axis=0, concat_axis=0, tiled...  7.33 us
    pallas_call x1, Pallas kernels, one_stage(): pl.pallas_call(functools.partial(tokens_kernel, pitch=pitch, block=block)...  6.31 us
    all_to_all x1, waiting for transfers between devices, one_stage(): lax.all_to_all(pieces, ('lat', 'lon'), split_axis=0, concat_axis=0, tiled...  3.43 us
    pallas_call x1, Pallas kernels, one_stage(): pl.pallas_call(functools.partial(windows_kernel, lat_count=lat_count, lon...  2.12 us
  transfers between devices with their start and end apart: 1, of which 1 were waited for; matrix products, arithmetic and copies ran while one was open for 0% of the time, Pallas kernels for 44%

profile of v5, /device:TPU:0, one launch (start us, length us, event | category | flops | bytes accessed | tf_op | source)
XLA Modules:
  0.0 34.4 jit_solution(6435057322662002730)
XLA Ops:
  0.0 2.1 %windows.1 = bf16[32,7,4,368]{3,2,1,0:T(4,128)(2,1)} custom-call(bf16[1,160,1440]{2,1,0:T(8,128)(2,1)} %raw_hbm.1), custom_call_target="tpu_custom_call" | custom-call | tf_op jit(solution)/shard_map/windows/pallas_call | solution.py:312
  2.1 7.3 %all-to-all-start = ((bf16[32,7,4,368]{3,2,1,0:T(4,128)(2,1)}), bf16[32,7,4,368]{3,2,1,0:T(4,128)(2,1)S(1)}, u32[]{:S(2)}, u32[]{:S(2)}) async-start(bf16[32,7,4,368]{3,2,1,0:T(4,128)(2,1)} %windows.1), calls=%async_computation | async-start | bytes 1376256 | tf_op jit(solution)/shard_map/all_to_all | solution.py:327
  9.5 15.1 %compose.1 = (bf16[2,512,1024]{2,1,0:T(8,128)(2,1)S(1)}, bf16[7,512,1024]{2,1,0:T(8,128)(2,1)}, f32[3,8,1024]{2,1,0:T(8,128)S(1)}, f32[2,8,128]{2,1,0:T(8,128)S(1)}) custom-call(bf16[32,4,4,1024]{3,2,1,0:T(4,128)(2,1)} %embed_hbm.1, f32[1,1024]{1,0:T(1,128)} %bitcast.4, f32[1,1024]{1,0:T(1,128)} %bitcast.5, bf16[9,1024,1024]{2,1,0:T(8,128)(2,1)} %bitcast.3), custom_call_target="tpu_custom_call" | custom-call | tf_op jit(solution)/shard_map/compose/pallas_call | solution.py:333
  24.6 3.4 %all-to-all-done.tile_ref = bf16[32,7,4,368]{3,2,1,0:T(4,128)(2,1)S(1)} async-done(((bf16[32,7,4,368]{3,2,1,0:T(4,128)(2,1)}), bf16[32,7,4,368]{3,2,1,0:T(4,128)(2,1)S(1)}, u32[]{:S(2)}, u32[]{:S(2)}) %all-to-all-start) | async-done | bytes 659488 | tf_op jit(solution)/shard_map/all_to_all | solution.py:327
  28.0 6.3 %tokens.1 = bf16[5,90,1024]{2,1,0:T(8,128)(2,1)} custom-call(bf16[32,7,4,368]{3,2,1,0:T(4,128)(2,1)S(1)} %all-to-all-done.tile_ref, bf16[2,512,1024]{2,1,0:T(8,128)(2,1)S(1)} %get-tuple-element.9.near_ref, bf16[7,512,1024]{2,1,0:T(8,128)(2,1)} %get-tuple-element.10.far_hbm, f32[3,8,1024]{2,1,0:T(8,128)S(1)} %get-tuple-element.11.bias_ref, ...), custom_call_target="tpu_custom_call" | custom-call | tf_op jit(solution)/shard_map/tokens/pallas_call | solution.py:370
Async XLA Ops:
  2.1 25.9 %all-to-all-start = ((bf16[32,7,4,368]{3,2,1,0:T(4,128)(2,1)}), bf16[32,7,4,368]{3,2,1,0:T(4,128)(2,1)S(1)}, u32[]{:S(2)}, u32[]{:S(2)}) async-start(bf16[32,7,4,368]{3,2,1,0:T(4,128)(2,1)} %windows.1), calls=%async_computation | async-start | bytes 1376256 | tf_op jit(solution)/shard_map/all_to_all | solution.py:327
